TPU v7x, 128 devices: a whole 4x4x4 slice. The times are simulated.
128 devices in a mesh: dp: 4 (over y), ctx: 32 (over x, z, core).
Axes of the slice: x: 4, y: 4, z: 4, core: 2. Of those that a mesh axis runs over, the one named last changes fastest.
Arguments:
- tokens: bfloat16 [32768, 1024], P(('dp', 'ctx')), parts along dimension 0, may hold values from -48 to 48
- w_query: bfloat16 [1024, 1024], replicated
- w_key: bfloat16 [1024, 1024], replicated
- w_value: bfloat16 [1024, 1024], replicated, may hold values from -0.1875 to 0.1875
- w_out: bfloat16 [1024, 1024], replicated, may hold values from -0.5 to 0.5
- norm_gain: float32 [1024], replicated, may hold values from 0.5 to 1.5
- norm_bias: float32 [1024], replicated, may hold values from -4 to 4
- w_pool: bfloat16 [1024, 1024], replicated, may hold values from -0.1875 to 0.1875
- pool_bias: float32 [1024], replicated, may hold values from -6 to 6
- random_ids: int32 [512, 16, 3], P(('dp', 'ctx')), parts along dimension 0, may hold values from 0 to 127, as said below
- lengths: int32 [32], P('dp'), parts along dimension 0, may hold values from 1 to 2048, 8192 in all
Outputs:
- encoded: bfloat16 [32768, 1024], P(('dp', 'ctx')), parts along dimension 0
- doc_vectors: float32 [32, 1024], P('dp'), parts along dimension 0
There are 4 independent parts, one for each index of `dp`. A program takes and returns all parts, laid end to end along the dimension named above; an argument that names none is the same for every part. Nothing has to cross between parts.
Inputs may be any that keep to these rules, and one draw needn't show every extreme that they name: `random_ids`: entry [b, h, r] is the key block of the r-th random block of query block b and head h. Among the 192 entries of the rows of one device, at most 8 name blocks of the range i * 4 to (i + 1) * 4 - 1 of any one device i; in every draw some device's range is named by exactly 8 entries of the rows of every device.
All inputs are finite; a program needn't handle non-finite values.
Results may differ from a plain program's by a relative error of at most 0.0089.
Values may be sent and summed in bfloat16 or wider, within the bound.
A program may use at most 128 MiB of HBM per device.

v0:
```python
import jax
import jax.numpy as jnp
from jax import lax
from jax.sharding import PartitionSpec as P

HEADS = 16
BLK = 64
RAND = 3
masked_score = -30000.0


def with_halo(cells, sides, width):
    for axis, dim in sides:
        count = lax.axis_size(axis)
        ends = count - 1
        head = lax.slice_in_dim(cells, 0, width, axis=dim)
        tail = lax.slice_in_dim(cells, cells.shape[dim] - width, cells.shape[dim], axis=dim)
        cells = jnp.concatenate(
            [
                lax.ppermute(tail, axis, [(i, (i + 1) % count) for i in range(ends)]),
                cells,
                lax.ppermute(head, axis, [((i + 1) % count, i) for i in range(ends)]),
            ],
            axis=dim,
        )
    return cells


def doc_number(positions, doc_ends):
    return jnp.sum((positions[..., None] >= doc_ends).astype(jnp.int32), axis=-1)


def partial_attention(
    queries, keys_in, values_in, query_pos, key_pos, doc_ends, seq_total, by_document
):
    score_scale = queries.shape[-1] ** (-0.5)
    scores = (
        jnp.einsum("...qd,...kd->...qk", queries, keys_in, preferred_element_type=jnp.float32)
        * score_scale
    )
    inside = ((key_pos >= 0) & (key_pos < seq_total))[..., None, :]
    if by_document:
        same_doc = (
            doc_number(query_pos, doc_ends)[..., :, None]
            == doc_number(key_pos, doc_ends)[..., None, :]
        )
        inside = same_doc & inside
    scores = jnp.where(inside, scores, masked_score)
    row_max = jnp.max(scores, axis=-1)
    weights = jnp.exp(scores - row_max[..., None])
    row_total = jnp.sum(weights, axis=-1)
    partial_out = jnp.einsum(
        "...qk,...kd->...qd",
        weights.astype(jnp.bfloat16),
        values_in,
        preferred_element_type=jnp.float32,
    )
    return (row_max, row_total, partial_out)


def combine(win_parts, rand_parts):
    win_max, win_total, win_out = win_parts
    rand_max, rand_total, rand_out = rand_parts
    joint_max = jnp.maximum(win_max, jnp.max(rand_max, axis=2))
    win_scale = jnp.exp(win_max - joint_max)
    rand_scale = jnp.exp(rand_max - joint_max[:, :, None])
    numerator = win_scale[..., None] * win_out + jnp.sum(rand_scale[..., None] * rand_out, axis=2)
    denominator = win_scale * win_total + jnp.sum(rand_scale * rand_total, axis=2)
    return (numerator / denominator[..., None]).astype(jnp.bfloat16)


def head_blocks(rows):
    return rows.reshape(-1, BLK, HEADS, rows.shape[1] // HEADS).transpose(0, 2, 1, 3)


def per_device(
    tokens,
    w_query,
    w_key,
    w_value,
    w_out,
    norm_gain,
    norm_bias,
    w_pool,
    pool_bias,
    random_ids,
    lengths,
):
    shards = lax.axis_size("ctx")
    own_index = lax.axis_index("ctx")
    tok_rows, model_width = tokens.shape
    head_dim = model_width // HEADS
    blocks = tok_rows // BLK
    seq_total = tok_rows * shards
    first_block = own_index * blocks
    doc_ends = jnp.cumsum(lengths)
    queries = jnp.dot(tokens, w_query, preferred_element_type=jnp.float32).astype(jnp.bfloat16)
    keys_rows = jnp.dot(tokens, w_key, preferred_element_type=jnp.float32).astype(jnp.bfloat16)
    values_rows = jnp.dot(tokens, w_value, preferred_element_type=jnp.float32).astype(jnp.bfloat16)
    query_blocks = head_blocks(queries)
    keys_blocks = head_blocks(keys_rows)
    values_blocks = head_blocks(values_rows)
    paired = jnp.concatenate((keys_rows, values_rows), axis=1)
    paired_ext = with_halo(paired, (("ctx", 0),), BLK)
    keys_ext = paired_ext[:, :model_width]
    values_ext = paired_ext[:, model_width:]
    keys_ext_blocks = head_blocks(keys_ext)
    values_ext_blocks = head_blocks(values_ext)
    window_keys = jnp.concatenate(
        (keys_ext_blocks[:-2], keys_ext_blocks[1:-1], keys_ext_blocks[2:]), axis=2
    )
    window_values = jnp.concatenate(
        (values_ext_blocks[:-2], values_ext_blocks[1:-1], values_ext_blocks[2:]), axis=2
    )
    block_ids = first_block + jnp.arange(blocks, dtype=jnp.int32)
    query_pos = block_ids[:, None, None] * BLK + jnp.arange(BLK, dtype=jnp.int32)
    window_pos = (block_ids - 1)[:, None, None] * BLK + jnp.arange(3 * BLK, dtype=jnp.int32)
    win_parts = partial_attention(
        query_blocks, window_keys, window_values, query_pos, window_pos, doc_ends, seq_total, True
    )
    requests = HEADS * blocks * RAND
    capacity = max(2, (5 * requests + 4 * shards - 1) // (4 * shards))
    wanted = random_ids.reshape(requests)
    owners = wanted // blocks
    local_block = wanted % blocks
    one_hot = (owners[:, None] == jnp.arange(shards, dtype=jnp.int32)[None, :]).astype(jnp.int32)
    slot_index = jnp.sum((jnp.cumsum(one_hot, axis=0) - one_hot) * one_hot, axis=1)
    placed = owners * capacity + slot_index
    request_ids = jnp.arange(requests, dtype=jnp.int32)
    source = jnp.full((shards * capacity,), requests, jnp.int32).at[placed].set(request_ids)
    filled = source < requests
    picked = jnp.minimum(source, requests - 1)
    head_of = picked // RAND % HEADS
    block_size = BLK * head_dim
    shape_five = (blocks, HEADS, RAND, BLK, head_dim)
    query_rows = query_blocks.reshape(blocks * HEADS, block_size)
    sent_queries = jnp.where(filled[:, None], query_rows[picked // RAND], 0).reshape(
        shards, capacity, block_size
    )
    sent_meta = jnp.stack(
        (head_of, local_block[picked], first_block + picked // (RAND * HEADS)), axis=1
    )
    sent_meta = jnp.where(filled[:, None], sent_meta, 0).reshape(shards, capacity, 3)
    got_queries = lax.all_to_all(sent_queries, "ctx", split_axis=0, concat_axis=0, tiled=True)
    got_meta = lax.all_to_all(sent_meta, "ctx", split_axis=0, concat_axis=0, tiled=True)
    count = got_queries.shape[1]
    heads_in = got_meta[..., 0]
    blocks_in = got_meta[..., 1]
    anchor = got_meta[..., 2]
    asked_queries = got_queries.reshape(shards, count, BLK, head_dim)
    asked_keys = keys_blocks[blocks_in, heads_in]
    asked_values = values_blocks[blocks_in, heads_in]
    asked_qpos = anchor[..., None] * BLK + jnp.arange(BLK, dtype=jnp.int32)
    asked_kpos = ((first_block + blocks_in) * BLK)[..., None] + jnp.arange(BLK, dtype=jnp.int32)
    row_max, row_total, partial_out = partial_attention(
        asked_queries, asked_keys, asked_values, asked_qpos, asked_kpos, doc_ends, seq_total, False
    )
    got_out = lax.all_to_all(
        partial_out.reshape(shards, count, block_size),
        "ctx",
        split_axis=0,
        concat_axis=0,
        tiled=True,
    )
    got_max = lax.all_to_all(row_max, "ctx", split_axis=0, concat_axis=0, tiled=True)
    got_total = lax.all_to_all(row_total, "ctx", split_axis=0, concat_axis=0, tiled=True)
    rand_max = got_max.reshape(shards * capacity, BLK)[placed].reshape(blocks, HEADS, RAND, BLK)
    rand_total = got_total.reshape(shards * capacity, BLK)[placed].reshape(blocks, HEADS, RAND, BLK)
    rand_out = got_out.reshape(shards * capacity, block_size)[placed].reshape(shape_five)
    rand_parts = (rand_max, rand_total, rand_out)
    attention = combine(win_parts, rand_parts)
    attn_rows = attention.transpose(0, 2, 1, 3).reshape(tok_rows, model_width)
    mixed = tokens.astype(jnp.float32) + jnp.dot(
        attn_rows, w_out, preferred_element_type=jnp.float32
    )
    centre = jnp.mean(mixed, axis=1, keepdims=True)
    spread = jnp.mean(jnp.square(mixed - centre), axis=1, keepdims=True)
    encoded = ((mixed - centre) * lax.rsqrt(spread + 1e-05) * norm_gain + norm_bias).astype(
        jnp.bfloat16
    )
    starts = doc_ends - lengths
    positions = own_index * tok_rows + jnp.arange(tok_rows, dtype=jnp.int32)
    chooser = (starts[:, None] == positions[None, :]).astype(jnp.bfloat16)
    local_rows = jnp.dot(chooser, encoded, preferred_element_type=jnp.float32)
    pooled = lax.psum(local_rows.astype(jnp.bfloat16), "ctx")
    doc_vectors = jnp.tanh(jnp.dot(pooled, w_pool, preferred_element_type=jnp.float32) + pool_bias)
    return (encoded, doc_vectors)


def solution(mesh):
    placed = (
        P(("dp", "ctx"), None),
        P(),
        P(),
        P(),
        P(),
        P(),
        P(),
        P(),
        P(),
        P(("dp", "ctx"), None, None),
        P("dp"),
    )
    return jax.shard_map(
        per_device,
        mesh=mesh,
        in_specs=placed,
        out_specs=(P(("dp", "ctx"), None), P("dp", None)),
        check_vma=False,
    )
```

profile of v0, /device:TPU:0, one launch (start us, length us, event | category | flops | bytes accessed | tf_op | source)
XLA Modules:
  0.0 346.8 jit_solution(10397523645476951693)
XLA Ops:
  4.3 2.0 gather_fusion
  7.5 8.3 %all-to-all-start = ((s32[32,8,3]{1,2,0:T(4,128)}), s32[32,8,3]{1,2,0:T(4,128)S(1)}, u32[]{:S(2)}, u32[]{:S(2)}) async-start(s32[32,8,3]{1,2,0:T(4,128)} %copy.74), calls=%async_computation | async-start | bytes 131072 | tf_op jit(solution)/shard_map/all_to_all | solution.py:145
  15.8 3.3 convolution_convert_fusion.2
  19.0 1.8 reshape.387
  20.8 1.3 copy.93
  22.1 2.1 reshape.393
  24.2 3.2 gather_fusion.1
  27.4 3.2 bitcast_select_fusion
  30.6 7.7 %all-to-all-start.1 = ((bf16[32,8,4096]{2,1,0:T(8,128)(2,1)}), bf16[32,8,4096]{2,1,0:T(8,128)(2,1)}, u32[]{:S(2)}, u32[]{:S(2)}) async-start(bf16[32,8,4096]{2,1,0:T(8,128)(2,1)} %bitcast_select_fusion), calls=%async_computation.1 | async-start | bytes 4194304 | tf_op jit(solution)/shard_map/all_to_all | solution.py:144
  38.3 2.3 convolution_convert_fusion.1
  41.4 1.7 reshape.395
  43.1 1.5 copy.92
  44.6 3.3 convolution_convert_fusion
  48.1 3.3 gather_fusion.2
  51.5 15.5 %all-to-all-done.1 = bf16[32,8,4096]{2,1,0:T(8,128)(2,1)} async-done(((bf16[32,8,4096]{2,1,0:T(8,128)(2,1)}), bf16[32,8,4096]{2,1,0:T(8,128)(2,1)}, u32[]{:S(2)}, u32[]{:S(2)}) %all-to-all-start.1) | async-done | bytes 2097184 | tf_op jit(solution)/shard_map/all_to_all | solution.py:144
  67.0 6.9 %reshape.394 = bf16[32,8,64,64]{3,2,1,0:T(8,128)(2,1)} reshape(bf16[32,8,4096]{2,1,0:T(8,128)(2,1)} %all-to-all-done.1) | data formatting | bytes 4194304 | tf_op jit(solution)/shard_map/reshape | solution.py:150
  73.9 5.4 %fusion = (f32[32,8,64]{2,1,0:T(8,128)S(1)}, f32[32,8,64,64]{2,3,1,0:T(8,128)S(1)}) fusion(pred[32,8,64]{2,1,0:T(8,128)(4,1)S(1)} %fusion.38, bf16[32,8,64,64]{3,2,1,0:T(8,128)(2,1)} %reshape.394, bf16[32,8,64,64]{3,2,1,0:T(8,128)(2,1)} %bitcast.84), kind=kOutput, calls=%fused_computation.10 | convolution fusion | flops 137347072 | bytes 8470528 | tf_op jit(solution)/shard_map/...qd,...kd->...qk/dot_general | solution.py:38
  79.3 3.2 copy-done.1
  82.5 3.7 %fusion.1 = f32[32,8,64]{2,1,0:T(8,128)S(1)} fusion(f32[32,8,64,64]{2,3,1,0:T(8,128)S(1)} %get-tuple-element.25, f32[32,8,64]{2,1,0:T(8,128)S(1)} %get-tuple-element.24, pred[32,8,64]{2,1,0:T(8,128)(4,1)S(1)} %fusion.38), kind=kLoop, calls=%fused_computation.11 | loop fusion | flops 4177920 | bytes 4341760 | tf_op jit(solution)/shard_map/reduce_sum | solution.py:51
  87.0 3.9 %all-to-all-start.4 = ((f32[32,1,512]{2,1,0:T(1,128)}), f32[32,1,512]{2,1,0:T(1,128)S(1)}, u32[]{:S(2)}, u32[]{:S(2)}) async-start(f32[32,1,512]{2,1,0:T(1,128)} %reshape.481), calls=%async_computation.4 | async-start | bytes 131072 | tf_op jit(solution)/shard_map/all_to_all | solution.py:166
  91.7 1.3 collective-permute-start.1
  93.0 3.8 %collective-permute-start = (bf16[64,2048]{1,0:T(8,128)(2,1)}, bf16[64,2048]{1,0:T(8,128)(2,1)}, u32[]{:S(2)}, u32[]{:S(2)}) collective-permute-start(bf16[64,2048]{1,0:T(8,128)(2,1)} %get-tuple-element.16), channel_id=1, source_target_pairs={{0,1},{1,2},{2,3},{3,4},{4,5},{5,6},{6,7},{7,8},{8,9},{9,10},{10,1... | collective-permute-start | bytes 786440 | tf_op jit(solution)/shard_map/ppermute | solution.py:20
  96.7 1.7 reshape.399
  98.5 1.5 copy.91
  100.0 3.3 gather_fusion.4
  104.0 9.5 %all-to-all-start.2 = ((f32[32,1,512]{2,1,0:T(1,128)}), f32[32,1,512]{2,1,0:T(1,128)S(1)}, u32[]{:S(2)}, u32[]{:S(2)}) async-start(f32[32,1,512]{2,1,0:T(1,128)} %reshape.479), calls=%async_computation.2 | async-start | bytes 131072 | tf_op jit(solution)/shard_map/all_to_all | solution.py:165
  113.5 10.6 %fusion.3 = f32[32,8,64,64]{3,2,1,0:T(8,128)} fusion(bf16[32,8,64,64]{3,2,1,0:T(8,128)(2,1)} %bitcast.83, f32[32,8,64,64]{2,3,1,0:T(8,128)} %copy-done.1, f32[32,8,64]{2,1,0:T(8,128)S(1)} %get-tuple-element.24, pred[32,8,64]{2,1,0:T(8,128)(4,1)S(1)} %fusion.38), kind=kOutput, calls=%fused_computation.14 | convolution fusion | flops 138412032 | bytes 10567680 | tf_op jit(solution)/shard_map/...qk,...kd->...qd/dot_general | solution.py:52
  124.1 7.9 %reshape.400 = f32[32,8,4096]{2,1,0:T(8,128)} reshape(f32[32,8,64,64]{3,2,1,0:T(8,128)} %fusion.3) | data formatting | bytes 8388608 | tf_op jit(solution)/shard_map/reshape | solution.py:159
  132.7 7.7 %all-to-all-start.3 = ((f32[32,8,4096]{2,1,0:T(8,128)}), f32[32,8,4096]{2,1,0:T(8,128)}, u32[]{:S(2)}, u32[]{:S(2)}) async-start(f32[32,8,4096]{2,1,0:T(8,128)} %reshape.400), calls=%async_computation.3 | async-start | bytes 8388608 | tf_op jit(solution)/shard_map/all_to_all | solution.py:158
  143.4 3.2 reshape.388
  146.6 3.2 copy.65
  149.8 1.9 reshape.398
  151.7 3.2 copy.76
  154.9 2.8 fusion.65
  157.8 2.1 fusion.63
  159.9 2.0 fusion.9
  161.9 1.9 copy-done.8
  163.8 2.1 fusion.10
  168.1 1.6 reduce.9
  172.3 20.4 %all-to-all-done.3 = f32[32,8,4096]{2,1,0:T(8,128)} async-done(((f32[32,8,4096]{2,1,0:T(8,128)}), f32[32,8,4096]{2,1,0:T(8,128)}, u32[]{:S(2)}, u32[]{:S(2)}) %all-to-all-start.3) | async-done | bytes 4194336 | tf_op jit(solution)/shard_map/all_to_all | solution.py:158
  192.7 6.8 %gather_fusion.5 = f32[192,4096]{1,0:T(8,128)} fusion(f32[256,4096]{1,0:T(8,128)} %bitcast.18, s32[1024]{0:T(1024)S(1)} %pad_clamp_fusion), kind=kCustom, calls=%fused_computation.5 | custom fusion | bytes 6292224 | tf_op jit(solution)/shard_map/gather | solution.py:169
  199.4 6.1 %reshape.402 = f32[4,16,3,64,64]{4,3,2,1,0:T(8,128)} reshape(f32[192,4096]{1,0:T(8,128)} %gather_fusion.5) | data formatting | bytes 6291456 | tf_op jit(solution)/shard_map/reshape | solution.py:169
  205.6 5.4 %multiply_reduce_fusion = f32[4,16,64,64]{3,2,1,0:T(8,128)S(1)} fusion(f32[4,16,3,64,64]{4,3,2,1,0:T(8,128)} %reshape.402, f32[4,16,3,64]{3,2,1,0:T(4,128)S(1)} %get-tuple-element.5), kind=kLoop, calls=%fused_computation.13 | loop fusion | flops 1310720 | bytes 4243456 | tf_op jit(solution)/shard_map/reduce_sum | solution.py:67
  211.0 3.3 fusion.26
  215.0 1.5 reshape.405
  216.6 2.0 fusion.66
  219.3 124.9 %psum.7 = bf16[8,1024]{1,0:T(8,128)(2,1)S(1)} all-reduce(bf16[8,1024]{1,0:T(8,128)(2,1)S(1)} %convolution_convert_fusion.3), channel_id=1, replica_groups=mesh['dp'=4,'ctx'=32] {'ctx'}, use_global_device_ids=true, to_apply=%region_16.17 | all-reduce | flops 8192 | bytes 32768 | tf_op jit(solution)/shard_map/psum | solution.py:185
  344.2 2.6 fusion.31
  (121 shorter events, 17.9 us)
Async XLA Ops:
  0.6 215.9 %copy-start = (bf16[1024,1024]{1,0:T(8,128)(2,1)S(1)}, bf16[1024,1024]{1,0:T(8,128)(2,1)}, u32[]{:S(2)}) copy-start(bf16[1024,1024]{1,0:T(8,128)(2,1)} %param.15) | copy-start | bytes 6291460
  7.5 23.1 %all-to-all-start = ((s32[32,8,3]{1,2,0:T(4,128)}), s32[32,8,3]{1,2,0:T(4,128)S(1)}, u32[]{:S(2)}, u32[]{:S(2)}) async-start(s32[32,8,3]{1,2,0:T(4,128)} %copy.74), calls=%async_computation | async-start | bytes 131072 | tf_op jit(solution)/shard_map/all_to_all | solution.py:145
  20.8 1.3 copy-start.10
  27.4 10.9 %copy-start.15 = (bf16[256,1024]{1,0:T(8,128)(2,1)S(1)}, bf16[256,1024]{1,0:T(8,128)(2,1)}, u32[]{:S(2)}) copy-start(bf16[256,1024]{1,0:T(8,128)(2,1)} %param.11) | copy-start | bytes 1572868
  30.6 36.4 %all-to-all-start.1 = ((bf16[32,8,4096]{2,1,0:T(8,128)(2,1)}), bf16[32,8,4096]{2,1,0:T(8,128)(2,1)}, u32[]{:S(2)}, u32[]{:S(2)}) async-start(bf16[32,8,4096]{2,1,0:T(8,128)(2,1)} %bitcast_select_fusion), calls=%async_computation.1 | async-start | bytes 4194304 | tf_op jit(solution)/shard_map/all_to_all | solution.py:144
  40.6 0.8 copy-start.3
  79.3 3.2 copy-start.1
  82.5 8.4 %copy-start.4 = (bf16[256,1024]{1,0:T(8,128)(2,1)S(1)}, bf16[256,1024]{1,0:T(8,128)(2,1)}, u32[]{:S(2)}) copy-start(bf16[256,1024]{1,0:T(8,128)(2,1)} %copy-done.3) | copy-start | bytes 1572868
  82.5 8.4 %copy-start.6 = (bf16[256,1024]{1,0:T(8,128)(2,1)S(1)}, bf16[256,1024]{1,0:T(8,128)(2,1)}, u32[]{:S(2)}) copy-start(bf16[256,1024]{1,0:T(8,128)(2,1)} %convolution_convert_fusion) | copy-start | bytes 1572868
  87.0 17.1 %all-to-all-start.4 = ((f32[32,1,512]{2,1,0:T(1,128)}), f32[32,1,512]{2,1,0:T(1,128)S(1)}, u32[]{:S(2)}, u32[]{:S(2)}) async-start(f32[32,1,512]{2,1,0:T(1,128)} %reshape.481), calls=%async_computation.4 | async-start | bytes 131072 | tf_op jit(solution)/shard_map/all_to_all | solution.py:166
  91.7 49.4 %collective-permute-start.1 = (bf16[64,2048]{1,0:T(8,128)(2,1)}, bf16[64,2048]{1,0:T(8,128)(2,1)}, u32[]{:S(2)}, u32[]{:S(2)}) collective-permute-start(bf16[64,2048]{1,0:T(8,128)(2,1)} %get-tuple-element.17), channel_id=1, source_target_pairs={{1,0},{2,1},{3,2},{4,3},{5,4},{6,5},{7,6},{8,7},{9,8},{10,9},{11,1... | collective-permute-start | bytes 786440 | tf_op jit(solution)/shard_map/ppermute | solution.py:22
  93.0 48.2 %collective-permute-start = (bf16[64,2048]{1,0:T(8,128)(2,1)}, bf16[64,2048]{1,0:T(8,128)(2,1)}, u32[]{:S(2)}, u32[]{:S(2)}) collective-permute-start(bf16[64,2048]{1,0:T(8,128)(2,1)} %get-tuple-element.16), channel_id=1, source_target_pairs={{0,1},{1,2},{2,3},{3,4},{4,5},{5,6},{6,7},{7,8},{8,9},{9,10},{10,1... | collective-permute-start | bytes 786440 | tf_op jit(solution)/shard_map/ppermute | solution.py:20
  104.0 28.0 %all-to-all-start.2 = ((f32[32,1,512]{2,1,0:T(1,128)}), f32[32,1,512]{2,1,0:T(1,128)S(1)}, u32[]{:S(2)}, u32[]{:S(2)}) async-start(f32[32,1,512]{2,1,0:T(1,128)} %reshape.479), calls=%async_computation.2 | async-start | bytes 131072 | tf_op jit(solution)/shard_map/all_to_all | solution.py:165
  132.0 8.4 %copy-start.25 = (s32[8]{0:T(128)S(1)}, s32[8]{0:T(128)}, u32[]{:S(2)}) copy-start(s32[8]{0:T(128)} %param.21) | copy-start | bytes 100
  132.0 9.1 %copy-start.5 = (bf16[256,1024]{1,0:T(8,128)(2,1)S(1)}, bf16[256,1024]{1,0:T(8,128)(2,1)}, u32[]{:S(2)}) copy-start(bf16[256,1024]{1,0:T(8,128)(2,1)} %copy-done.3) | copy-start | bytes 1572868
  132.0 9.1 %copy-start.7 = (bf16[256,1024]{1,0:T(8,128)(2,1)S(1)}, bf16[256,1024]{1,0:T(8,128)(2,1)}, u32[]{:S(2)}) copy-start(bf16[256,1024]{1,0:T(8,128)(2,1)} %convolution_convert_fusion) | copy-start | bytes 1572868
  132.0 0.6 copy-start.21
  132.7 60.0 %all-to-all-start.3 = ((f32[32,8,4096]{2,1,0:T(8,128)}), f32[32,8,4096]{2,1,0:T(8,128)}, u32[]{:S(2)}, u32[]{:S(2)}) async-start(f32[32,8,4096]{2,1,0:T(8,128)} %reshape.400), calls=%async_computation.3 | async-start | bytes 8388608 | tf_op jit(solution)/shard_map/all_to_all | solution.py:158
  141.1 20.8 %copy-start.19 = (pred[4,64,192]{2,1,0:T(8,128)(4,1)}, pred[4,64,192]{2,1,0:T(8,128)(4,1)S(1)}, u32[]{:S(2)}) copy-start(pred[4,64,192]{2,1,0:T(8,128)(4,1)S(1)} %compare_and_fusion) | copy-start | bytes 147460
  154.9 2.8 copy-start.2
  157.7 2.1 copy-start.11
  161.9 2.0 copy-start.8
  161.9 8.8 %copy-start.16 = (f32[4,16,64]{2,1,0:T(8,128)}, f32[4,16,64]{2,1,0:T(8,128)S(1)}, u32[]{:S(2)}) copy-start(f32[4,16,64]{2,1,0:T(8,128)S(1)} %get-tuple-element.26) | copy-start | bytes 49156
  170.7 0.6 copy-start.18
  205.5 5.4 %copy-start.9 = (f32[4,16,64,192]{3,2,1,0:T(8,128)S(1)}, f32[4,16,64,192]{3,2,1,0:T(8,128)}, u32[]{:S(2)}) copy-start(f32[4,16,64,192]{3,2,1,0:T(8,128)} %copy-done.8) | copy-start | bytes 9437188
  205.5 5.4 %copy-start.13 = (bf16[4,16,64,64]{2,3,1,0:T(8,128)(2,1)S(1)}, bf16[4,16,64,64]{2,3,1,0:T(8,128)(2,1)}, u32[]{:S(2)}) copy-start(bf16[4,16,64,64]{2,3,1,0:T(8,128)(2,1)} %get-tuple-element.9) | copy-start | bytes 1572868
  205.5 5.4 %copy-start.14 = (bf16[4,16,64,64]{2,3,1,0:T(8,128)(2,1)S(1)}, bf16[4,16,64,64]{2,3,1,0:T(8,128)(2,1)}, u32[]{:S(2)}) copy-start(bf16[4,16,64,64]{2,3,1,0:T(8,128)(2,1)} %get-tuple-element.10) | copy-start | bytes 1572868
  205.5 5.5 %copy-start.17 = (f32[4,16,64]{2,1,0:T(8,128)S(1)}, f32[4,16,64]{2,1,0:T(8,128)}, u32[]{:S(2)}) copy-start(f32[4,16,64]{2,1,0:T(8,128)} %copy-done.16) | copy-start | bytes 49156
  205.5 5.5 %copy-start.20 = (pred[4,64,192]{2,1,0:T(8,128)(4,1)S(1)}, pred[4,64,192]{2,1,0:T(8,128)(4,1)}, u32[]{:S(2)}) copy-start(pred[4,64,192]{2,1,0:T(8,128)(4,1)} %copy-done.19) | copy-start | bytes 147460
  214.3 4.5 %copy-start.22 = (f32[1024]{0:T(1024)S(1)}, f32[1024]{0:T(1024)}, u32[]{:S(2)}) copy-start(f32[1024]{0:T(1024)} %param.17) | copy-start | bytes 12292
  214.3 4.5 %copy-start.23 = (f32[1024]{0:T(1024)S(1)}, f32[1024]{0:T(1024)}, u32[]{:S(2)}) copy-start(f32[1024]{0:T(1024)} %param.16) | copy-start | bytes 12292
  215.0 129.2 %copy-start.24 = (f32[1024]{0:T(1024)S(1)}, f32[1024]{0:T(1024)}, u32[]{:S(2)}) copy-start(f32[1024]{0:T(1024)} %param.19) | copy-start | bytes 12292
  219.1 127.7 %copy-start.12 = (bf16[256,1024]{1,0:T(8,128)(2,1)}, bf16[256,1024]{1,0:T(8,128)(2,1)S(1)}, u32[]{:S(2)}) copy-start(bf16[256,1024]{1,0:T(8,128)(2,1)S(1)} %add_convert_fusion) | copy-start | bytes 1572868
where the time goes:
time: 348 us; the launch traced here: 347 us
  blocking collectives  125 us (36%)
  local copies, waits for them, and re-layouts  85.6 us (25%)
  starting transfers between devices  42.1 us (12%)
  waiting for transfers between devices  35.9 us (10%)
  matrix products  34.9 us (10%)
  other arithmetic  22.2 us (6%)
    psum x1, blocking collectives, per_device(): pooled = lax.psum(local_rows.astype(jnp.bfloat16), 'ctx')  125 us
    reshape x10, local copies, waits for them, and re-layouts, head_blocks(): rows.reshape(-1, BLK, HEADS, rows.shape[1] // HEADS).transpose(0, 2, 1, 3)  21 us
    all_to_all x1, waiting for transfers between devices, per_device(): lax.all_to_all(partial_out.reshape(shards, count, block_size), 'ctx', spl...  20.4 us
    all_to_all x1, waiting for transfers between devices, per_device(): lax.all_to_all(sent_queries, 'ctx', split_axis=0, concat_axis=0, tiled=True)  15.5 us
    dot_general x2, matrix products, partial_attention(): jnp.einsum('...qk,...kd->...qd', weights.astype(jnp.bfloat16), values_in,...  13.9 us
    unnamed x57, local copies, waits for them, and re-layouts  9.87 us
    all_to_all x1, starting transfers between devices, per_device(): lax.all_to_all(row_max, 'ctx', split_axis=0, concat_axis=0, tiled=True)  9.47 us
    all_to_all x1, starting transfers between devices, per_device(): lax.all_to_all(sent_meta, 'ctx', split_axis=0, concat_axis=0, tiled=True)  8.28 us
  transfers between devices with their start and end apart: 7, of which 2 were waited for; matrix products, arithmetic and copies ran while one was open for 24% of the time, Pallas kernels for 0%

commit v1 on v0

--- a/solution.py
+++ b/solution.py
@@ -182,7 +182,9 @@
     positions = own_index * tok_rows + jnp.arange(tok_rows, dtype=jnp.int32)
     chooser = (starts[:, None] == positions[None, :]).astype(jnp.bfloat16)
     local_rows = jnp.dot(chooser, encoded, preferred_element_type=jnp.float32)
-    pooled = lax.psum(local_rows.astype(jnp.bfloat16), "ctx")
+    part = local_rows.astype(jnp.bfloat16)
+    shards_2 = lax.all_gather(part, "ctx", axis=0, tiled=False)
+    pooled = shards_2.sum(axis=0)
     doc_vectors = jnp.tanh(jnp.dot(pooled, w_pool, preferred_element_type=jnp.float32) + pool_bias)
     return (encoded, doc_vectors)
 

time: 348 us -> 248 us (0.71)
  blocking collectives: 125 us -> 24.5 us
    psum x1 -> x0, blocking collectives: 125 us -> none  [per_device(): pooled = lax.psum(local_rows.astype(jnp.bfloat16), 'ctx')]
    all_gather x0 -> x1, blocking collectives: none -> 24.5 us  [per_device(): shards_2 = lax.all_gather(part, 'ctx', axis=0, tiled=False)]
    unnamed x57 -> x59, local copies, waits for them, and re-layouts: 9.87 us -> 9.87 us
  transfers between devices with their start and end apart: 7 -> 7, of which waited for: 2 -> 2; matrix products, arithmetic and copies ran while one was open for 24% -> 34% of each run, Pallas kernels for 0% -> 0%
where the time goes in v1:
time: 248 us; the launch traced here: 245 us
  local copies, waits for them, and re-layouts  85.6 us (35%)
  starting transfers between devices  42.1 us (17%)
  waiting for transfers between devices  35.9 us (14%)
  matrix products  33.5 us (14%)
  blocking collectives  24.5 us (10%)
  other arithmetic  22.3 us (9%)
    all_gather x1, blocking collectives, per_device(): shards_2 = lax.all_gather(part, 'ctx', axis=0, tiled=False)  24.5 us
    reshape x10, local copies, waits for them, and re-layouts, head_blocks(): rows.reshape(-1, BLK, HEADS, rows.shape[1] // HEADS).transpose(0, 2, 1, 3)  21 us
    all_to_all x1, waiting for transfers between devices, per_device(): lax.all_to_all(partial_out.reshape(shards, count, block_size), 'ctx', spl...  20.4 us
    all_to_all x1, waiting for transfers between devices, per_device(): lax.all_to_all(sent_queries, 'ctx', split_axis=0, concat_axis=0, tiled=True)  15.5 us
    dot_general x2, matrix products, partial_attention(): jnp.einsum('...qk,...kd->...qd', weights.astype(jnp.bfloat16), values_in,...  13.9 us
    unnamed x59, local copies, waits for them, and re-layouts  9.87 us
    all_to_all x1, starting transfers between devices, per_device(): lax.all_to_all(row_max, 'ctx', split_axis=0, concat_axis=0, tiled=True)  9.47 us
    all_to_all x1, starting transfers between devices, per_device(): lax.all_to_all(sent_meta, 'ctx', split_axis=0, concat_axis=0, tiled=True)  8.28 us
  transfers between devices with their start and end apart: 7, of which 2 were waited for; matrix products, arithmetic and copies ran while one was open for 34% of the time, Pallas kernels for 0%

profile of v1, /device:TPU:0, one launch (start us, length us, event | category | flops | bytes accessed | tf_op | source)
XLA Modules:
  0.0 245.1 jit_solution(12745410935672095798)
XLA Ops:
  2.9 1.2 scatter_custom_fusion
  4.3 2.0 gather_fusion
  7.5 8.3 %all-to-all-start = ((s32[32,8,3]{1,2,0:T(4,128)}), s32[32,8,3]{1,2,0:T(4,128)S(1)}, u32[]{:S(2)}, u32[]{:S(2)}) async-start(s32[32,8,3]{1,2,0:T(4,128)} %copy.74), calls=%async_computation | async-start | bytes 131072 | tf_op jit(solution)/shard_map/all_to_all | solution.py:145
  15.8 3.3 %convolution_convert_fusion.2 = bf16[256,1024]{1,0:T(8,128)(2,1)} fusion(bf16[256,1024]{1,0:T(8,128)(2,1)} %param.11, bf16[1024,1024]{1,0:T(8,128)(2,1)} %param.12), kind=kOutput, calls=%fused_computation.49 | convolution fusion | flops 537133056 | bytes 3145728 | tf_op jit(solution)/shard_map/dot_general | solution.py:97
  19.0 1.8 reshape.387
  20.8 1.3 copy.93
  22.1 2.1 reshape.393
  24.2 3.2 %gather_fusion.1 = bf16[256,4096]{1,0:T(8,128)(2,1)} fusion(bf16[64,4096]{1,0:T(8,128)(2,1)S(1)} %reshape.393, s32[1024]{0:T(1024)S(1)} %get-tuple-element.32), kind=kCustom, calls=%fused_computation.1 | custom fusion | bytes 4195328 | tf_op jit(solution)/shard_map/gather | solution.py:137
  27.4 3.2 %bitcast_select_fusion = bf16[32,8,4096]{2,1,0:T(8,128)(2,1)} fusion(bf16[256,4096]{1,0:T(8,128)(2,1)} %gather_fusion.1, pred[32,8]{1,0:T(8,128)(4,1)S(1)} %broadcast_in_dim.52), kind=kLoop, calls=%fused_computation.40 | loop fusion | flops 1048576 | bytes 4194560 | tf_op jit(solution)/shard_map/jit(_where)/select_n | solution.py:137
  30.6 7.7 %all-to-all-start.1 = ((bf16[32,8,4096]{2,1,0:T(8,128)(2,1)}), bf16[32,8,4096]{2,1,0:T(8,128)(2,1)}, u32[]{:S(2)}, u32[]{:S(2)}) async-start(bf16[32,8,4096]{2,1,0:T(8,128)(2,1)} %bitcast_select_fusion), calls=%async_computation.1 | async-start | bytes 4194304 | tf_op jit(solution)/shard_map/all_to_all | solution.py:144
  38.3 2.3 convolution_convert_fusion.1
  41.4 1.7 reshape.395
  43.1 1.5 copy.92
  44.6 3.3 %convolution_convert_fusion = bf16[256,1024]{1,0:T(8,128)(2,1)} fusion(bf16[256,1024]{1,0:T(8,128)(2,1)} %param.11, bf16[1024,1024]{1,0:T(8,128)(2,1)} %param.14), kind=kOutput, calls=%fused_computation.47 | convolution fusion | flops 537133056 | bytes 3145728 | tf_op jit(solution)/shard_map/dot_general | solution.py:99
  48.1 3.3 %gather_fusion.2 = bf16[256,64,64]{2,1,0:T(8,128)(2,1)} fusion(bf16[4,16,64,64]{3,2,1,0:T(8,128)(2,1)S(1)} %bitcast.83, s32[256]{0:T(256)S(1)} %reshape.423), kind=kCustom, calls=%fused_computation.2 | custom fusion | bytes 4196352 | tf_op jit(solution)/shard_map/gather | solution.py:151
  51.5 15.5 %all-to-all-done.1 = bf16[32,8,4096]{2,1,0:T(8,128)(2,1)} async-done(((bf16[32,8,4096]{2,1,0:T(8,128)(2,1)}), bf16[32,8,4096]{2,1,0:T(8,128)(2,1)}, u32[]{:S(2)}, u32[]{:S(2)}) %all-to-all-start.1) | async-done | bytes 2097184 | tf_op jit(solution)/shard_map/all_to_all | solution.py:144
  67.0 6.9 %reshape.394 = bf16[32,8,64,64]{3,2,1,0:T(8,128)(2,1)} reshape(bf16[32,8,4096]{2,1,0:T(8,128)(2,1)} %all-to-all-done.1) | data formatting | bytes 4194304 | tf_op jit(solution)/shard_map/reshape | solution.py:150
  73.9 5.4 %fusion = (f32[32,8,64]{2,1,0:T(8,128)S(1)}, f32[32,8,64,64]{2,3,1,0:T(8,128)S(1)}) fusion(pred[32,8,64]{2,1,0:T(8,128)(4,1)S(1)} %fusion.38, bf16[32,8,64,64]{3,2,1,0:T(8,128)(2,1)} %reshape.394, bf16[32,8,64,64]{3,2,1,0:T(8,128)(2,1)} %bitcast.86), kind=kOutput, calls=%fused_computation.10 | convolution fusion | flops 137347072 | bytes 8470528 | tf_op jit(solution)/shard_map/...qd,...kd->...qk/dot_general | solution.py:38
  79.3 3.2 %copy-done.1 = f32[32,8,64,64]{2,3,1,0:T(8,128)} copy-done((f32[32,8,64,64]{2,3,1,0:T(8,128)}, f32[32,8,64,64]{2,3,1,0:T(8,128)S(1)}, u32[]{:S(2)}) %copy-start.1) | copy-done | bytes 4194328
  82.5 3.7 %fusion.1 = f32[32,8,64]{2,1,0:T(8,128)S(1)} fusion(f32[32,8,64,64]{2,3,1,0:T(8,128)S(1)} %get-tuple-element.25, f32[32,8,64]{2,1,0:T(8,128)S(1)} %get-tuple-element.24, pred[32,8,64]{2,1,0:T(8,128)(4,1)S(1)} %fusion.38), kind=kLoop, calls=%fused_computation.11 | loop fusion | flops 4177920 | bytes 4341760 | tf_op jit(solution)/shard_map/reduce_sum | solution.py:51
  87.0 3.9 %all-to-all-start.4 = ((f32[32,1,512]{2,1,0:T(1,128)}), f32[32,1,512]{2,1,0:T(1,128)S(1)}, u32[]{:S(2)}, u32[]{:S(2)}) async-start(f32[32,1,512]{2,1,0:T(1,128)} %reshape.482), calls=%async_computation.4 | async-start | bytes 131072 | tf_op jit(solution)/shard_map/all_to_all | solution.py:166
  91.7 1.3 collective-permute-start.1
  93.0 3.8 %collective-permute-start = (bf16[64,2048]{1,0:T(8,128)(2,1)}, bf16[64,2048]{1,0:T(8,128)(2,1)}, u32[]{:S(2)}, u32[]{:S(2)}) collective-permute-start(bf16[64,2048]{1,0:T(8,128)(2,1)} %get-tuple-element.16), channel_id=1, source_target_pairs={{0,1},{1,2},{2,3},{3,4},{4,5},{5,6},{6,7},{7,8},{8,9},{9,10},{10,1... | collective-permute-start | bytes 786440 | tf_op jit(solution)/shard_map/ppermute | solution.py:20
  96.7 1.7 reshape.399
  98.5 1.5 copy.91
  100.0 3.3 %gather_fusion.4 = bf16[256,64,64]{2,1,0:T(8,128)(2,1)} fusion(bf16[4,16,64,64]{3,2,1,0:T(8,128)(2,1)S(1)} %bitcast.84, s32[256]{0:T(256)S(1)} %reshape.423), kind=kCustom, calls=%fused_computation.4 | custom fusion | bytes 4196352 | tf_op jit(solution)/shard_map/gather | solution.py:152
  104.0 9.5 %all-to-all-start.2 = ((f32[32,1,512]{2,1,0:T(1,128)}), f32[32,1,512]{2,1,0:T(1,128)S(1)}, u32[]{:S(2)}, u32[]{:S(2)}) async-start(f32[32,1,512]{2,1,0:T(1,128)} %reshape.480), calls=%async_computation.2 | async-start | bytes 131072 | tf_op jit(solution)/shard_map/all_to_all | solution.py:165
  113.5 10.6 %fusion.3 = f32[32,8,64,64]{3,2,1,0:T(8,128)} fusion(bf16[32,8,64,64]{3,2,1,0:T(8,128)(2,1)} %bitcast.85, f32[32,8,64,64]{2,3,1,0:T(8,128)} %copy-done.1, f32[32,8,64]{2,1,0:T(8,128)S(1)} %get-tuple-element.24, pred[32,8,64]{2,1,0:T(8,128)(4,1)S(1)} %fusion.38), kind=kOutput, calls=%fused_computation.14 | convolution fusion | flops 138412032 | bytes 10567680 | tf_op jit(solution)/shard_map/...qk,...kd->...qd/dot_general | solution.py:52
  124.1 7.9 %reshape.400 = f32[32,8,4096]{2,1,0:T(8,128)} reshape(f32[32,8,64,64]{3,2,1,0:T(8,128)} %fusion.3) | data formatting | bytes 8388608 | tf_op jit(solution)/shard_map/reshape | solution.py:159
  132.7 7.7 %all-to-all-start.3 = ((f32[32,8,4096]{2,1,0:T(8,128)}), f32[32,8,4096]{2,1,0:T(8,128)}, u32[]{:S(2)}, u32[]{:S(2)}) async-start(f32[32,8,4096]{2,1,0:T(8,128)} %reshape.400), calls=%async_computation.3 | async-start | bytes 8388608 | tf_op jit(solution)/shard_map/all_to_all | solution.py:158
  143.4 3.2 %reshape.388 = bf16[6,64,16,64]{3,2,1,0:T(8,128)(2,1)} reshape(bf16[384,1024]{1,0:T(8,128)(2,1)} %get-tuple-element.12) | data formatting | bytes 1572864 | tf_op jit(solution)/shard_map/reshape | solution.py:73
  146.6 3.2 %copy.65 = bf16[6,64,16,64]{1,3,2,0:T(8,128)(2,1)} copy(bf16[6,64,16,64]{3,2,1,0:T(8,128)(2,1)} %reshape.388) | data formatting | bytes 1572864 | tf_op jit(solution)/shard_map/reshape | solution.py:73
  149.8 1.9 reshape.398
  151.7 3.2 %copy.76 = bf16[6,64,16,64]{1,3,2,0:T(8,128)(2,1)} copy(bf16[6,64,16,64]{3,2,1,0:T(8,128)(2,1)} %reshape.398) | data formatting | bytes 1572864 | tf_op jit(solution)/shard_map/reshape | solution.py:73
  154.9 2.8 %fusion.65 = (bf16[4,16,64,64]{2,3,1,0:T(8,128)(2,1)S(1)}, bf16[4,16,64,64]{2,3,1,0:T(8,128)(2,1)S(1)}, bf16[4,16,64,64]{2,3,1,0:T(8,128)(2,1)S(1)}) fusion(bf16[6,16,64,64]{2,3,1,0:T(8,128)(2,1)} %bitcast.87), kind=kLoop, calls=%fused_computation.143 | loop fusion | bytes 3145728 | tf_op jit(solution)/shard_map/slice | solution.py:110
  157.8 2.1 fusion.63
  159.9 2.0 fusion.9
  161.9 1.9 copy-done.8
  163.8 2.1 fusion.10
  168.1 1.6 reduce.10
  172.3 20.4 %all-to-all-done.3 = f32[32,8,4096]{2,1,0:T(8,128)} async-done(((f32[32,8,4096]{2,1,0:T(8,128)}), f32[32,8,4096]{2,1,0:T(8,128)}, u32[]{:S(2)}, u32[]{:S(2)}) %all-to-all-start.3) | async-done | bytes 4194336 | tf_op jit(solution)/shard_map/all_to_all | solution.py:158
  192.7 6.8 %gather_fusion.5 = f32[192,4096]{1,0:T(8,128)} fusion(f32[256,4096]{1,0:T(8,128)} %bitcast.18, s32[1024]{0:T(1024)S(1)} %pad_clamp_fusion), kind=kCustom, calls=%fused_computation.5 | custom fusion | bytes 6292224 | tf_op jit(solution)/shard_map/gather | solution.py:169
  199.4 6.1 %reshape.402 = f32[4,16,3,64,64]{4,3,2,1,0:T(8,128)} reshape(f32[192,4096]{1,0:T(8,128)} %gather_fusion.5) | data formatting | bytes 6291456 | tf_op jit(solution)/shard_map/reshape | solution.py:169
  205.6 5.4 %multiply_reduce_fusion = f32[4,16,64,64]{3,2,1,0:T(8,128)S(1)} fusion(f32[4,16,3,64,64]{4,3,2,1,0:T(8,128)} %reshape.402, f32[4,16,3,64]{3,2,1,0:T(4,128)S(1)} %get-tuple-element.5), kind=kLoop, calls=%fused_computation.13 | loop fusion | flops 1310720 | bytes 4243456 | tf_op jit(solution)/shard_map/reduce_sum | solution.py:67
  211.0 3.3 %fusion.26 = bf16[4,64,16,64]{3,1,2,0:T(8,128)(2,1)S(1)} fusion(f32[4,16,64,64]{3,2,1,0:T(8,128)S(1)} %multiply_reduce_fusion, f32[4,64,16]{1,2,0:T(8,128)S(1)} %get-tuple-element.2, f32[4,64,16]{1,2,0:T(8,128)S(1)} %get-tuple-element.3, bf16[4,16,64,64]{2,3,1,0:T(8,128)(2,1)S(1)} %copy-done.14, bf16[4,16,64,64]{2,3,1,0:T(8,128)(2,1)S(1)} %copy-done.15, ...), kind=kOutput, calls=%fused_computation.38 | convolution fusion | flops 109576192 | bytes 6389760 | tf_op jit(solution)/shard_map/...qk,...kd->...qd/dot_general | solution.py:52
  215.0 1.5 reshape.405
  216.5 2.1 fusion.66
  219.5 24.5 %all-gather = bf16[256,1024]{1,0:T(8,128)(2,1)S(1)} all-gather(bf16[8,1024]{1,0:T(8,128)(2,1)S(1)} %convolution_convert_fusion.3), channel_id=2, replica_groups=mesh['dp'=4,'ctx'=32] {'ctx'}, dimensions={0}, use_global_device_ids=true | all-gather | bytes 540672 | tf_op jit(solution)/shard_map/all_gather | solution.py:186
  (124 shorter events, 17.8 us)
Async XLA Ops:
  0.6 215.9 %copy-start = (bf16[1024,1024]{1,0:T(8,128)(2,1)S(1)}, bf16[1024,1024]{1,0:T(8,128)(2,1)}, u32[]{:S(2)}) copy-start(bf16[1024,1024]{1,0:T(8,128)(2,1)} %param.15) | copy-start | bytes 6291460
  7.5 23.1 %all-to-all-start = ((s32[32,8,3]{1,2,0:T(4,128)}), s32[32,8,3]{1,2,0:T(4,128)S(1)}, u32[]{:S(2)}, u32[]{:S(2)}) async-start(s32[32,8,3]{1,2,0:T(4,128)} %copy.74), calls=%async_computation | async-start | bytes 131072 | tf_op jit(solution)/shard_map/all_to_all | solution.py:145
  20.8 1.3 copy-start.10
  27.4 10.9 %copy-start.16 = (bf16[256,1024]{1,0:T(8,128)(2,1)S(1)}, bf16[256,1024]{1,0:T(8,128)(2,1)}, u32[]{:S(2)}) copy-start(bf16[256,1024]{1,0:T(8,128)(2,1)} %param.11) | copy-start | bytes 1572868
  30.6 36.4 %all-to-all-start.1 = ((bf16[32,8,4096]{2,1,0:T(8,128)(2,1)}), bf16[32,8,4096]{2,1,0:T(8,128)(2,1)}, u32[]{:S(2)}, u32[]{:S(2)}) async-start(bf16[32,8,4096]{2,1,0:T(8,128)(2,1)} %bitcast_select_fusion), calls=%async_computation.1 | async-start | bytes 4194304 | tf_op jit(solution)/shard_map/all_to_all | solution.py:144
  40.6 0.8 copy-start.3
  79.3 3.2 %copy-start.1 = (f32[32,8,64,64]{2,3,1,0:T(8,128)}, f32[32,8,64,64]{2,3,1,0:T(8,128)S(1)}, u32[]{:S(2)}) copy-start(f32[32,8,64,64]{2,3,1,0:T(8,128)S(1)} %get-tuple-element.25) | copy-start | bytes 12582916
  82.5 8.4 %copy-start.4 = (bf16[256,1024]{1,0:T(8,128)(2,1)S(1)}, bf16[256,1024]{1,0:T(8,128)(2,1)}, u32[]{:S(2)}) copy-start(bf16[256,1024]{1,0:T(8,128)(2,1)} %copy-done.3) | copy-start | bytes 1572868
  82.5 8.4 %copy-start.6 = (bf16[256,1024]{1,0:T(8,128)(2,1)S(1)}, bf16[256,1024]{1,0:T(8,128)(2,1)}, u32[]{:S(2)}) copy-start(bf16[256,1024]{1,0:T(8,128)(2,1)} %convolution_convert_fusion) | copy-start | bytes 1572868
  87.0 17.1 %all-to-all-start.4 = ((f32[32,1,512]{2,1,0:T(1,128)}), f32[32,1,512]{2,1,0:T(1,128)S(1)}, u32[]{:S(2)}, u32[]{:S(2)}) async-start(f32[32,1,512]{2,1,0:T(1,128)} %reshape.482), calls=%async_computation.4 | async-start | bytes 131072 | tf_op jit(solution)/shard_map/all_to_all | solution.py:166
  91.7 49.4 %collective-permute-start.1 = (bf16[64,2048]{1,0:T(8,128)(2,1)}, bf16[64,2048]{1,0:T(8,128)(2,1)}, u32[]{:S(2)}, u32[]{:S(2)}) collective-permute-start(bf16[64,2048]{1,0:T(8,128)(2,1)} %get-tuple-element.17), channel_id=1, source_target_pairs={{1,0},{2,1},{3,2},{4,3},{5,4},{6,5},{7,6},{8,7},{9,8},{10,9},{11,1... | collective-permute-start | bytes 786440 | tf_op jit(solution)/shard_map/ppermute | solution.py:22
  93.0 48.2 %collective-permute-start = (bf16[64,2048]{1,0:T(8,128)(2,1)}, bf16[64,2048]{1,0:T(8,128)(2,1)}, u32[]{:S(2)}, u32[]{:S(2)}) collective-permute-start(bf16[64,2048]{1,0:T(8,128)(2,1)} %get-tuple-element.16), channel_id=1, source_target_pairs={{0,1},{1,2},{2,3},{3,4},{4,5},{5,6},{6,7},{7,8},{8,9},{9,10},{10,1... | collective-permute-start | bytes 786440 | tf_op jit(solution)/shard_map/ppermute | solution.py:20
  104.0 28.0 %all-to-all-start.2 = ((f32[32,1,512]{2,1,0:T(1,128)}), f32[32,1,512]{2,1,0:T(1,128)S(1)}, u32[]{:S(2)}, u32[]{:S(2)}) async-start(f32[32,1,512]{2,1,0:T(1,128)} %reshape.480), calls=%async_computation.2 | async-start | bytes 131072 | tf_op jit(solution)/shard_map/all_to_all | solution.py:165
  132.0 8.4 %copy-start.26 = (s32[8]{0:T(128)S(1)}, s32[8]{0:T(128)}, u32[]{:S(2)}) copy-start(s32[8]{0:T(128)} %param.21) | copy-start | bytes 100
  132.0 9.1 %copy-start.5 = (bf16[256,1024]{1,0:T(8,128)(2,1)S(1)}, bf16[256,1024]{1,0:T(8,128)(2,1)}, u32[]{:S(2)}) copy-start(bf16[256,1024]{1,0:T(8,128)(2,1)} %copy-done.3) | copy-start | bytes 1572868
  132.0 9.1 %copy-start.7 = (bf16[256,1024]{1,0:T(8,128)(2,1)S(1)}, bf16[256,1024]{1,0:T(8,128)(2,1)}, u32[]{:S(2)}) copy-start(bf16[256,1024]{1,0:T(8,128)(2,1)} %convolution_convert_fusion) | copy-start | bytes 1572868
  132.0 0.6 copy-start.22
  132.7 60.0 %all-to-all-start.3 = ((f32[32,8,4096]{2,1,0:T(8,128)}), f32[32,8,4096]{2,1,0:T(8,128)}, u32[]{:S(2)}, u32[]{:S(2)}) async-start(f32[32,8,4096]{2,1,0:T(8,128)} %reshape.400), calls=%async_computation.3 | async-start | bytes 8388608 | tf_op jit(solution)/shard_map/all_to_all | solution.py:158
  141.1 20.8 %copy-start.20 = (pred[4,64,192]{2,1,0:T(8,128)(4,1)}, pred[4,64,192]{2,1,0:T(8,128)(4,1)S(1)}, u32[]{:S(2)}) copy-start(pred[4,64,192]{2,1,0:T(8,128)(4,1)S(1)} %compare_and_fusion) | copy-start | bytes 147460
  154.9 2.8 %copy-start.2 = (bf16[6,64,16,64]{1,3,2,0:T(8,128)(2,1)S(1)}, bf16[6,64,16,64]{1,3,2,0:T(8,128)(2,1)}, u32[]{:S(2)}) copy-start(bf16[6,64,16,64]{1,3,2,0:T(8,128)(2,1)} %copy.76) | copy-start | bytes 2359300
  157.7 2.1 copy-start.11
  161.9 2.0 copy-start.8
  161.9 8.8 %copy-start.17 = (f32[4,16,64]{2,1,0:T(8,128)}, f32[4,16,64]{2,1,0:T(8,128)S(1)}, u32[]{:S(2)}) copy-start(f32[4,16,64]{2,1,0:T(8,128)S(1)} %get-tuple-element.26) | copy-start | bytes 49156
  170.7 0.6 copy-start.19
  205.5 5.4 %copy-start.9 = (f32[4,16,64,192]{3,2,1,0:T(8,128)S(1)}, f32[4,16,64,192]{3,2,1,0:T(8,128)}, u32[]{:S(2)}) copy-start(f32[4,16,64,192]{3,2,1,0:T(8,128)} %copy-done.8) | copy-start | bytes 9437188
  205.5 5.4 %copy-start.14 = (bf16[4,16,64,64]{2,3,1,0:T(8,128)(2,1)S(1)}, bf16[4,16,64,64]{2,3,1,0:T(8,128)(2,1)}, u32[]{:S(2)}) copy-start(bf16[4,16,64,64]{2,3,1,0:T(8,128)(2,1)} %get-tuple-element.9) | copy-start | bytes 1572868
  205.5 5.4 %copy-start.15 = (bf16[4,16,64,64]{2,3,1,0:T(8,128)(2,1)S(1)}, bf16[4,16,64,64]{2,3,1,0:T(8,128)(2,1)}, u32[]{:S(2)}) copy-start(bf16[4,16,64,64]{2,3,1,0:T(8,128)(2,1)} %get-tuple-element.10) | copy-start | bytes 1572868
  205.5 5.5 %copy-start.18 = (f32[4,16,64]{2,1,0:T(8,128)S(1)}, f32[4,16,64]{2,1,0:T(8,128)}, u32[]{:S(2)}) copy-start(f32[4,16,64]{2,1,0:T(8,128)} %copy-done.17) | copy-start | bytes 49156
  205.5 5.5 %copy-start.21 = (pred[4,64,192]{2,1,0:T(8,128)(4,1)S(1)}, pred[4,64,192]{2,1,0:T(8,128)(4,1)}, u32[]{:S(2)}) copy-start(pred[4,64,192]{2,1,0:T(8,128)(4,1)} %copy-done.20) | copy-start | bytes 147460
  214.3 4.7 %copy-start.23 = (f32[1024]{0:T(1024)S(1)}, f32[1024]{0:T(1024)}, u32[]{:S(2)}) copy-start(f32[1024]{0:T(1024)} %param.17) | copy-start | bytes 12292
  214.3 4.7 %copy-start.24 = (f32[1024]{0:T(1024)S(1)}, f32[1024]{0:T(1024)}, u32[]{:S(2)}) copy-start(f32[1024]{0:T(1024)} %param.16) | copy-start | bytes 12292
  216.5 27.5 %copy-start.12 = (bf16[1024,1024]{1,0:T(8,128)(2,1)S(1)}, bf16[1024,1024]{1,0:T(8,128)(2,1)}, u32[]{:S(2)}) copy-start(bf16[1024,1024]{1,0:T(8,128)(2,1)} %param.18) | copy-start | bytes 6291460
  216.5 27.5 %copy-start.25 = (f32[1024]{0:T(1024)S(1)}, f32[1024]{0:T(1024)}, u32[]{:S(2)}) copy-start(f32[1024]{0:T(1024)} %param.19) | copy-start | bytes 12292
  219.2 25.8 %copy-start.13 = (bf16[256,1024]{1,0:T(8,128)(2,1)}, bf16[256,1024]{1,0:T(8,128)(2,1)S(1)}, u32[]{:S(2)}) copy-start(bf16[256,1024]{1,0:T(8,128)(2,1)S(1)} %add_convert_fusion) | copy-start | bytes 1572868
